TPU v7x, 256 devices: a whole 4x4x8 slice. The times are simulated.
256 devices in a mesh: grp: 16 (over y_lo, z), mem: 16 (over y_hi, x, core).
Axes of the slice: x: 4, y: 4 (y_hi: 2, y_lo: 2; y = y_hi * 2 + y_lo), z: 8, core: 2. Of those that a mesh axis runs over, the one named last changes fastest.
Arguments:
- client_input: bfloat16 [16, 16, 128, 896], P('grp', 'mem'), may hold values from -6 to 6
- client_gain: float32 [16, 896], P('mem'), may hold values from 0.5 to 1.5
- w_query: bfloat16 [16, 896, 896], P('mem'), may hold values from -1.5 to 1.5
- w_keyval: bfloat16 [16, 896, 256], P('mem'), may hold values from -0.5 to 0.5
- w_out: bfloat16 [16, 896, 896], P('mem'), may hold values from -0.1875 to 0.1875
- server_gain: float32 [16, 896], P('grp'), may hold values from 0.5 to 1.5
- w_gate: bfloat16 [16, 896, 4864], P('grp', None, 'mem'), may hold values from -0.1875 to 0.1875
- w_up: bfloat16 [16, 896, 4864], P('grp', None, 'mem'), may hold values from -0.1875 to 0.1875
- w_down: bfloat16 [16, 4864, 896], P('grp', 'mem'), may hold values from -0.078125 to 0.078125
- out_grad: bfloat16 [16, 16, 128, 896], P('grp', 'mem'), may hold values from -6 to 6
- valid: int32 [16, 16], P('grp', 'mem'), may hold values from 64 to 128
Outputs:
- server_out: bfloat16 [16, 16, 128, 896], P('grp', 'mem')
- grad_query: bfloat16 [16, 896, 896], P('mem')
- grad_keyval: bfloat16 [16, 896, 256], P('mem')
- grad_out: bfloat16 [16, 896, 896], P('mem')
- grad_gate: bfloat16 [16, 896, 4864], P('grp', None, 'mem')
- grad_up: bfloat16 [16, 896, 4864], P('grp', None, 'mem')
- grad_down: bfloat16 [16, 4864, 896], P('grp', 'mem')
All inputs are finite; a program needn't handle non-finite values.
Results may differ from a plain program's by a relative error of at most 0.03.
Values may be sent and summed in bfloat16 or wider, within the bound.
A program may use at most 128 MiB of HBM per device.

v0:
```python
import jax
import jax.numpy as jnp
from jax import lax
from jax.sharding import PartitionSpec as P

KV_HEADS = 2
HEAD_DIM = 64
EPS = 1e-06


def side_by_side(arrays, axis, dim, along):
    widths = [a.shape[along] for a in arrays]
    both = jnp.concatenate(arrays, axis=along)
    filled = lax.all_gather(both, axis, axis=dim, tiled=True)
    return tuple(jnp.split(filled, [sum(widths[:k]) for k in range(1, len(widths))], axis=along))


def gathered_total(shard, axis):
    return lax.all_gather(shard, axis).astype(jnp.float32).sum(0)


def client_forward(tokens_in, gain_vec, query_w, keyval_w, output_w):
    x_float = tokens_in.astype(jnp.float32)
    inv_rms = lax.rsqrt(jnp.mean(x_float * x_float, axis=-1, keepdims=True) + EPS)
    normed = (x_float * inv_rms * gain_vec).astype(jnp.bfloat16)
    queries = jnp.dot(normed, query_w, preferred_element_type=jnp.float32).astype(jnp.bfloat16)
    key_vals = jnp.dot(normed, keyval_w, preferred_element_type=jnp.float32).astype(jnp.bfloat16)
    length = tokens_in.shape[0]
    half_cols = KV_HEADS * HEAD_DIM
    q_heads = queries.reshape(length, KV_HEADS, -1, HEAD_DIM)
    k_heads = key_vals[:, :half_cols].reshape(length, KV_HEADS, HEAD_DIM)
    v_heads = key_vals[:, half_cols:].reshape(length, KV_HEADS, HEAD_DIM)
    scores = jnp.einsum(
        "tgqd,sgd->gqts", q_heads, k_heads, preferred_element_type=jnp.float32
    ) * HEAD_DIM ** (-0.5)
    causal = jnp.arange(length)[:, None] >= jnp.arange(length)[None, :]
    scores = jnp.where(causal, scores, -1e30)
    highest = jnp.max(scores, axis=-1, keepdims=True)
    expo = jnp.exp(scores - highest)
    probs = (expo / jnp.sum(expo, axis=-1, keepdims=True)).astype(jnp.bfloat16)
    attended = jnp.einsum("gqts,sgd->tgqd", probs, v_heads, preferred_element_type=jnp.float32)
    attended = attended.astype(jnp.bfloat16).reshape(length, -1)
    mixed = jnp.dot(attended, output_w, preferred_element_type=jnp.float32)
    return (x_float + mixed).astype(jnp.bfloat16)


def norm_back(h_float, inv_rms, gain_vec, upstream):
    scaled = upstream * gain_vec
    return inv_rms * scaled - h_float * inv_rms**3 * jnp.mean(
        scaled * h_float, axis=-1, keepdims=True
    )


def on_device(
    client_input,
    client_gain,
    w_query,
    w_keyval,
    w_out,
    server_gain,
    w_gate,
    w_up,
    w_down,
    out_grad,
    valid,
):
    tokens_in = client_input[0, 0]
    gain_vec = client_gain[0]
    query_w = w_query[0]
    keyval_w = w_keyval[0]
    output_w = w_out[0]
    s_gain = server_gain[0]
    gate_w = w_gate[0]
    up_w = w_up[0]
    down_w = w_down[0]
    length = tokens_in.shape[0]
    width = tokens_in.shape[1]
    contract_last = (((1,), (1,)), ((), ()))
    contract_first = (((0,), (0,)), ((), ()))

    def client_part(query_in, keyval_in, output_in):
        return client_forward(tokens_in, gain_vec, query_in, keyval_in, output_in)

    own_cut, pull = jax.vjp(client_part, query_w, keyval_w, output_w)
    live = jnp.arange(length) < valid[0, 0]
    own_cot = jnp.where(live[:, None], out_grad[0, 0], jnp.zeros_like(out_grad[0, 0]))
    all_cut, all_cot = side_by_side((own_cut, own_cot), "mem", 0, 1)
    h_float = all_cut.astype(jnp.float32)
    inv_rms = lax.rsqrt(jnp.mean(h_float * h_float, axis=-1, keepdims=True) + EPS)
    normed = (h_float * inv_rms * s_gain).astype(jnp.bfloat16)
    gate_act = jnp.dot(normed, gate_w, preferred_element_type=jnp.float32)
    up_act = jnp.dot(normed, up_w, preferred_element_type=jnp.float32)
    sigma = jax.nn.sigmoid(gate_act)
    hidden = (gate_act * sigma * up_act).astype(jnp.bfloat16)
    served = lax.psum_scatter(
        jnp.dot(hidden, down_w, preferred_element_type=jnp.float32).astype(jnp.bfloat16),
        "mem",
        scatter_dimension=0,
        tiled=True,
    ).astype(jnp.float32)
    own_float = own_cut.astype(jnp.float32)
    server_out = (own_float + served).astype(jnp.bfloat16)
    d_hidden = lax.dot_general(all_cot, down_w, contract_last, preferred_element_type=jnp.float32)
    d_gate = (d_hidden * up_act * sigma * (1.0 + gate_act * (1.0 - sigma))).astype(jnp.bfloat16)
    d_up = (d_hidden * gate_act * sigma).astype(jnp.bfloat16)
    grad_down = lax.dot_general(
        hidden, all_cot, contract_first, preferred_element_type=jnp.float32
    ).astype(jnp.bfloat16)
    grad_gate = lax.dot_general(
        normed, d_gate, contract_first, preferred_element_type=jnp.float32
    ).astype(jnp.bfloat16)
    grad_up = lax.dot_general(
        normed, d_up, contract_first, preferred_element_type=jnp.float32
    ).astype(jnp.bfloat16)
    d_normed = lax.dot_general(d_gate, gate_w, contract_last, preferred_element_type=jnp.float32)
    d_normed = d_normed + lax.dot_general(
        d_up, up_w, contract_last, preferred_element_type=jnp.float32
    )
    pushed = norm_back(h_float, inv_rms, s_gain, d_normed)
    local_sum = jnp.sum(pushed.reshape(-1, length, width), axis=0) + own_cot.astype(jnp.float32)
    grad_total = gathered_total(local_sum.astype(jnp.bfloat16), "mem").astype(jnp.float32)
    cut_grad = (grad_total / lax.axis_size("mem")).astype(jnp.bfloat16)
    grad_q, grad_kv, grad_o = pull(cut_grad)
    summed = (
        lax.psum(grad_q.astype(jnp.float32).astype(jnp.bfloat16), "grp").astype(jnp.float32),
        lax.psum(grad_kv.astype(jnp.float32).astype(jnp.bfloat16), "grp").astype(jnp.float32),
        lax.psum(grad_o.astype(jnp.float32).astype(jnp.bfloat16), "grp").astype(jnp.float32),
    )
    groups = lax.axis_size("grp")
    grad_query = (summed[0] / groups).astype(jnp.bfloat16)
    grad_keyval = (summed[1] / groups).astype(jnp.bfloat16)
    grad_out = (summed[2] / groups).astype(jnp.bfloat16)
    return (
        server_out[None, None],
        grad_query[None],
        grad_keyval[None],
        grad_out[None],
        grad_gate[None],
        grad_up[None],
        grad_down[None],
    )


def solution(mesh):
    in_specs = (
        P("grp", "mem", None, None),
        P("mem", None),
        P("mem", None, None),
        P("mem", None, None),
        P("mem", None, None),
        P("grp", None),
        P("grp", None, "mem"),
        P("grp", None, "mem"),
        P("grp", "mem", None),
        P("grp", "mem", None, None),
        P("grp", "mem"),
    )
    out_specs = (
        P("grp", "mem", None, None),
        P("mem", None, None),
        P("mem", None, None),
        P("mem", None, None),
        P("grp", None, "mem"),
        P("grp", None, "mem"),
        P("grp", "mem", None),
    )
    return jax.shard_map(
        on_device, mesh=mesh, in_specs=in_specs, out_specs=out_specs, check_vma=False
    )
```

profile of v0, /device:TPU:2, one launch (start us, length us, event | category | flops | bytes accessed | tf_op | source)
XLA Modules:
  0.0 434.7 jit_solution(6634465796072064970)
XLA Ops:
  8.0 1.1 fusion.63
  9.8 1.4 convolution_convert_fusion.9
  11.5 2.1 fusion.29
  17.4 75.3 %all-gather.3.cloned.1.call-done = bf16[2048,1792]{1,0:T(8,128)(2,1)} async-done(((bf16[128,1792]{1,0:T(8,128)(2,1)}), bf16[2048,1792]{1,0:T(8,128)(2,1)}) %all-gather.3.cloned.1.call-update) | async-done | bytes 7340048 | tf_op jit(solution)/shard_map/all_gather | solution.py:14
  92.7 2.8 fusion
  95.6 2.6 fusion.2
  98.3 1.5 fusion.57
  100.1 1.5 fusion.61
  101.9 1.1 slice-done.1
  103.0 3.5 multiply_convert_fusion.2
  106.5 2.3 fusion.59
  108.8 3.4 fusion.5
  112.2 3.8 fusion.4
  116.0 4.2 reduce_sum.95
  120.2 1.9 fusion.69
  122.4 5.6 %convolution_convert_fusion = bf16[2048,896]{1,0:T(8,128)(2,1)} fusion(bf16[2048,304]{0,1:T(8,128)(2,1)} %get-tuple-element.14, bf16[1,304,896]{2,1,0:T(8,128)(2,1)} %param.19), kind=kOutput, calls=%fused_computation.12 | convolution fusion | flops 1117519872 | bytes 5459968 | tf_op jit(solution)/shard_map/dot_general | solution.py:96
  128.7 51.6 %all-gather.5.cloned.1.call-done = bf16[16,128,896]{2,1,0:T(8,128)(2,1)} async-done(((bf16[1,128,896]{2,1,0:T(8,128)(2,1)}), bf16[16,128,896]{2,1,0:T(8,128)(2,1)}) %all-gather.5.cloned.1.call-update) | async-done | bytes 3670032 | tf_op jit(solution)/shard_map/all_gather | solution.py:19
  180.3 2.6 convert_reduce_fusion
  183.6 1.3 fusion.32
  184.9 1.8 copy.37
  186.7 1.4 fusion.47
  189.7 1.2 convolution_convert_fusion.5
  191.1 1.8 convolution_convert_fusion.2
  192.9 1.7 convolution_convert_fusion.1
  194.7 5.1 %fusion.22 = bf16[1,896,304]{1,2,0:T(8,128)(2,1)} fusion(bf16[2048,304]{0,1:T(8,128)(2,1)} %copy-done.11, bf16[2048,896]{1,0:T(8,128)(2,1)} %copy-done.4), kind=kOutput, calls=%fused_computation.43 | convolution fusion | flops 1115957248 | bytes 5459968 | tf_op jit(solution)/shard_map/dot_general | solution.py:112
  199.7 4.6 %fusion.21 = bf16[1,896,304]{1,2,0:T(8,128)(2,1)} fusion(bf16[2048,304]{0,1:T(8,128)(2,1)S(1)} %copy-done.6, bf16[2048,896]{1,0:T(8,128)(2,1)} %copy-done.4), kind=kOutput, calls=%fused_computation.42 | convolution fusion | flops 1115957248 | bytes 5459968 | tf_op jit(solution)/shard_map/dot_general | solution.py:109
  204.4 2.3 fusion.23
  206.6 62.0 %reduce-scatter.2.cloned.1.call-done = bf16[128,896]{1,0:T(8,128)(2,1)} async-done(((bf16[2048,896]{1,0:T(8,128)(2,1)}), bf16[128,896]{1,0:T(8,128)(2,1)}) %reduce-scatter.2.cloned.1.call-update) | async-done | bytes 229392 | tf_op jit(solution)/shard_map/reduce_scatter | solution.py:95
  268.6 1.7 fusion.72
  270.3 151.8 %all-reduce.5.cloned.1.call-done = (bf16[896,896]{1,0:T(8,128)(2,1)}, bf16[896,256]{1,0:T(8,128)(2,1)}, bf16[896,896]{1,0:T(8,128)(2,1)}) async-done(((bf16[896,896]{1,0:T(8,128)(2,1)}, bf16[896,256]{1,0:T(8,128)(2,1)}, bf16[896,896]{1,0:T(8,128)(2,1)}), (bf16[896,896]{1,0:T(8,128)(2,1)}, bf16[896,256]{1,0:T(8,128)(2,1)}, bf16[896,896]{1,0:T(8,128)(2,1)})) %all-reduce.5.cloned.1.call-update) | async-done | bytes 3670032 | tf_op jit(solution)/shard_map/psum | solution.py:125
  422.2 1.9 fusion.68
  424.0 4.2 fusion.10
  (90 shorter events, 8.9 us)
Async XLA Ops:
  7.2 8.0 %copy-start = (bf16[1,896,896]{2,1,0:T(8,128)(2,1)S(1)}, bf16[1,896,896]{2,1,0:T(8,128)(2,1)}, u32[]{:S(2)}) copy-start(bf16[1,896,896]{2,1,0:T(8,128)(2,1)} %param.15) | copy-start | bytes 4816900
  7.2 85.5 %all-gather.3.cloned.1.call-start = ((), (), s32[]{:S(2)}) async-start(), calls=%async_computation.1 | async-start | bytes 7798784 | tf_op jit(solution)/shard_map/all_gather | solution.py:14
  9.1 4.7 %copy-start.18 = (f32[128]{0:T(128)}, f32[128]{0:T(128)S(1)}, u32[]{:S(2)}) copy-start(f32[128]{0:T(128)S(1)} %add_rsqrt_fusion.1) | copy-start | bytes 1540
  9.8 4.0 copy-start.16
  13.6 1.3 copy-start.13
  13.8 0.7 copy-start.9
  13.8 1.4 copy-start.1
  14.8 2.6 copy-start.20
  15.7 0.7 copy-start.7
  17.2 163.1 %all-gather.5.cloned.1.call-start = ((), (), s32[]{:S(2)}) async-start(), calls=%async_computation.3 | async-start | bytes 3899392 | tf_op jit(solution)/shard_map/all_gather | solution.py:19
  95.6 2.6 copy-start.15
  98.2 1.9 copy-start.4
  98.2 1.9 copy-start.14
  98.2 3.7 slice-start
  100.1 2.9 slice-start.1
  100.1 2.9 copy-start.21
  106.5 2.3 copy-start.5
  106.5 2.3 copy-start.11
  122.1 146.5 %reduce-scatter.2.cloned.1.call-start = ((), (), s32[]{:S(2)}) async-start(), calls=%async_computation.2 | async-start | bytes 3899392 | tf_op jit(solution)/shard_map/reduce_scatter | solution.py:95
  128.0 294.2 %all-reduce.5.cloned.1.call-start = ((), (), s32[]{:S(2)}) async-start(), calls=%async_computation.4 | async-start | bytes 7340032 | tf_op jit(solution)/shard_map/psum | solution.py:125
  182.9 0.8 copy-start.2
  186.7 2.4 copy-start.10
  188.1 1.3 copy-start.12
  188.1 1.6 copy-start.17
  188.1 1.6 copy-start.19
  189.0 3.9 copy-start.3
  194.6 5.1 %copy-start.6 = (bf16[2048,304]{0,1:T(8,128)(2,1)S(1)}, bf16[2048,304]{0,1:T(8,128)(2,1)}, u32[]{:S(2)}) copy-start(bf16[2048,304]{0,1:T(8,128)(2,1)} %copy-done.5) | copy-start | bytes 3735556
  194.7 9.7 %slice-start.2 = ((s8[7340032]{0:T(1024)(128)(4,1)}), s8[4194304]{0:T(1024)(128)(4,1)S(1)}, s32[]{:S(2)}) async-start(s8[7340032]{0:T(1024)(128)(4,1)} %bitcast.184), calls=%async_computation.7 | async-start | bytes 8388608
  199.7 4.6 %slice-start.3 = ((s8[7340032]{0:T(1024)(128)(4,1)}), s8[3145728]{0:T(1024)(128)(4,1)S(1)}, s32[]{:S(2)}) async-start(s8[7340032]{0:T(1024)(128)(4,1)} %bitcast.184), calls=%async_computation.8 | async-start | bytes 6291456
  199.7 4.6 %copy-start.22 = (bf16[2048,304]{0,1:T(8,128)(2,1)S(1)}, bf16[2048,304]{0,1:T(8,128)(2,1)}, u32[]{:S(2)}) copy-start(bf16[2048,304]{0,1:T(8,128)(2,1)} %get-tuple-element.14) | copy-start | bytes 3735556
  204.4 64.3 %copy-start.8 = (bf16[128,896]{1,0:T(8,128)(2,1)S(1)}, bf16[128,896]{1,0:T(8,128)(2,1)}, u32[]{:S(2)}) copy-start(bf16[128,896]{1,0:T(8,128)(2,1)} %copy-done.7) | copy-start | bytes 688132
Sparse Core Ops, SparseCore 0:
  17.3 75.3 all-gather.2
  122.2 57.9 all-gather.4
  184.6 83.9 reduce-scatter.1
  272.0 150.1 all-reduce.4
where the time goes:
time: 435 us
  waiting for transfers between devices  341 us (78%)
  matrix products  42.4 us (10%)
  other arithmetic  30.3 us (7%)
  between operations  15 us (3%)
  local copies, waits for them, and re-layouts  5.74 us (1%)
    psum x1, waiting for transfers between devices, on_device(): lax.psum(grad_q.astype(jnp.float32).astype(jnp.bfloat16), 'grp')  152 us
    all_gather x1, waiting for transfers between devices, side_by_side(): filled = lax.all_gather(both, axis, axis=dim, tiled=True)  75.3 us
    reduce_scatter x1, waiting for transfers between devices, on_device(): lax.psum_scatter(jnp.dot(hidden, down_w, preferred_element_type=jnp.float...  62 us
    all_gather x1, waiting for transfers between devices, gathered_total(): return lax.all_gather(shard, axis).astype(jnp.float32).sum(0)  51.6 us
  transfers between devices with their start and end apart: 4, of which 4 were waited for; matrix products, arithmetic and copies ran while one was open for 8% of the time, Pallas kernels for 0%

commit v1 on v0

--- a/solution.py
+++ b/solution.py
@@ -6,6 +6,11 @@
 KV_HEADS = 2
 HEAD_DIM = 64
 EPS = 1e-06
+
+
+def add_all(value, mesh_axis):
+    parts = lax.all_gather(value, mesh_axis)
+    return jnp.sum(parts, axis=0)
 
 
 def side_by_side(arrays, axis, dim, along):
@@ -122,7 +127,7 @@
     cut_grad = (grad_total / lax.axis_size("mem")).astype(jnp.bfloat16)
     grad_q, grad_kv, grad_o = pull(cut_grad)
     summed = (
-        lax.psum(grad_q.astype(jnp.float32).astype(jnp.bfloat16), "grp").astype(jnp.float32),
+        add_all(grad_q.astype(jnp.float32).astype(jnp.bfloat16), "grp").astype(jnp.float32),
         lax.psum(grad_kv.astype(jnp.float32).astype(jnp.bfloat16), "grp").astype(jnp.float32),
         lax.psum(grad_o.astype(jnp.float32).astype(jnp.bfloat16), "grp").astype(jnp.float32),
     )

time: 435 us -> 709 us (1.63)
  waiting for transfers between devices: 341 us -> 603 us
  other arithmetic: 30.3 us -> 42.9 us
    all_gather x0 -> x1, waiting for transfers between devices: none -> 270 us  [add_all(): parts = lax.all_gather(value, mesh_axis)]
    reduce_sum x0 -> x1, other arithmetic: none -> 13.4 us  [add_all(): return jnp.sum(parts, axis=0)]
    psum x1, waiting for transfers between devices: 152 us -> 143 us  [on_device(): lax.psum(grad_kv.astype(jnp.float32).astype(jnp.bfloat16), 'grp')]
  transfers between devices with their start and end apart: 4 -> 5, of which waited for: 4 -> 5; matrix products, arithmetic and copies ran while one was open for 8% -> 5% of each run, Pallas kernels for 0% -> 0%
where the time goes in v1:
time: 709 us; the launch traced here: 708 us
  waiting for transfers between devices  603 us (85%)
  other arithmetic  42.9 us (6%)
  matrix products  42.4 us (6%)
  between operations  15.1 us (2%)
    all_gather x1, waiting for transfers between devices, add_all(): parts = lax.all_gather(value, mesh_axis)  270 us
    psum x1, waiting for transfers between devices, on_device(): lax.psum(grad_kv.astype(jnp.float32).astype(jnp.bfloat16), 'grp')  143 us
    all_gather x1, waiting for transfers between devices, side_by_side(): filled = lax.all_gather(both, axis, axis=dim, tiled=True)  75.3 us
    reduce_scatter x1, waiting for transfers between devices, on_device(): lax.psum_scatter(jnp.dot(hidden, down_w, preferred_element_type=jnp.float...  63.3 us
    all_gather x1, waiting for transfers between devices, gathered_total(): return lax.all_gather(shard, axis).astype(jnp.float32).sum(0)  51.7 us
  transfers between devices with their start and end apart: 5, of which 5 were waited for; matrix products, arithmetic and copies ran while one was open for 5% of the time, Pallas kernels for 0%

profile of v1, /device:TPU:2, one launch (start us, length us, event | category | flops | bytes accessed | tf_op | source)
XLA Modules:
  0.0 708.1 jit_solution(8471848691490064042)
XLA Ops:
  9.8 1.4 convolution_convert_fusion.9
  11.5 2.1 fusion.29
  17.2 75.3 %all-gather.5.cloned.1.call-done = bf16[2048,1792]{1,0:T(8,128)(2,1)} async-done(((bf16[128,1792]{1,0:T(8,128)(2,1)}), bf16[2048,1792]{1,0:T(8,128)(2,1)}) %all-gather.5.cloned.1.call-update) | async-done | bytes 7340048 | tf_op jit(solution)/shard_map/all_gather | solution.py:19
  92.5 2.8 fusion
  95.3 2.6 fusion.2
  98.0 1.5 fusion.57
  99.9 1.5 fusion.61
  102.8 3.5 multiply_convert_fusion.2
  106.2 2.3 fusion.59
  108.5 3.4 fusion.5
  111.9 3.7 fusion.4
  115.6 3.5 reduce_sum.107
  119.1 1.8 fusion.69
  121.2 5.5 convolution_convert_fusion
  127.4 51.7 %all-gather.7.cloned.1.call-done = bf16[16,128,896]{2,1,0:T(8,128)(2,1)} async-done(((bf16[1,128,896]{2,1,0:T(8,128)(2,1)}), bf16[16,128,896]{2,1,0:T(8,128)(2,1)}) %all-gather.7.cloned.1.call-update) | async-done | bytes 3670032 | tf_op jit(solution)/shard_map/all_gather | solution.py:24
  179.0 2.6 convert_reduce_fusion
  183.3 1.3 fusion.47
  185.8 1.2 fusion.38
  187.1 1.2 convolution_convert_fusion.5
  188.2 1.7 convolution_convert_fusion.1
  190.2 1.8 convolution_convert_fusion.2
  192.1 5.0 fusion.22
  197.1 4.6 fusion.21
  201.8 2.3 fusion.23
  204.1 63.3 %reduce-scatter.2.cloned.1.call-done = bf16[128,896]{1,0:T(8,128)(2,1)} async-done(((bf16[2048,896]{1,0:T(8,128)(2,1)}), bf16[128,896]{1,0:T(8,128)(2,1)}) %reduce-scatter.2.cloned.1.call-update) | async-done | bytes 229392 | tf_op jit(solution)/shard_map/reduce_scatter | solution.py:100
  267.4 1.7 fusion.72
  269.1 143.2 %all-reduce.5.cloned.1.call-done = (bf16[896,256]{1,0:T(8,128)(2,1)}, bf16[896,896]{1,0:T(8,128)(2,1)}) async-done(((bf16[896,256]{1,0:T(8,128)(2,1)}, bf16[896,896]{1,0:T(8,128)(2,1)}), (bf16[896,256]{1,0:T(8,128)(2,1)}, bf16[896,896]{1,0:T(8,128)(2,1)})) %all-reduce.5.cloned.1.call-update) | async-done | bytes 2064400 | tf_op jit(solution)/shard_map/psum | solution.py:131
  412.3 1.9 fusion.68
  414.1 2.9 fusion.11
  417.0 269.7 %all-gather.9.cloned.1.call-done = bf16[14336,896]{1,0:T(8,128)(2,1)} async-done(((bf16[896,896]{1,0:T(8,128)(2,1)}), bf16[14336,896]{1,0:T(8,128)(2,1)}) %all-gather.9.cloned.1.call-update) | async-done | bytes 25690128 | tf_op jit(solution)/shard_map/all_gather | solution.py:12
  686.7 13.4 %reduce_sum.113 = bf16[896,896]{1,0:T(8,128)(2,1)S(1)} reduce(bf16[16,896,896]{2,1,0:T(8,128)(2,1)} %bitcast.188, bf16[]{:T(256)} %constant.32.clone.1), dimensions={0}, to_apply=%region_11.12 | reduce | flops 12042240 | bytes 27295746 | tf_op jit(solution)/shard_map/reduce_sum | solution.py:13
  700.1 1.4 fusion.10
  (103 shorter events, 11.3 us)
Async XLA Ops:
  7.2 8.4 %copy-start = (bf16[1,896,896]{2,1,0:T(8,128)(2,1)S(1)}, bf16[1,896,896]{2,1,0:T(8,128)(2,1)}, u32[]{:S(2)}) copy-start(bf16[1,896,896]{2,1,0:T(8,128)(2,1)} %param.15) | copy-start | bytes 4816900
  7.2 85.3 %all-gather.5.cloned.1.call-start = ((), (), s32[]{:S(2)}) async-start(), calls=%async_computation.1 | async-start | bytes 7798784 | tf_op jit(solution)/shard_map/all_gather | solution.py:19
  9.1 4.7 copy-start.21
  9.8 4.0 copy-start.18
  11.2 3.3 copy-start.15
  11.5 4.1 copy-start.1
  14.3 2.8 copy-start.24
  16.1 81.9 %copy-start.9 = (bf16[128,896]{1,0:T(8,128)(2,1)}, bf16[128,896]{1,0:T(8,128)(2,1)S(1)}, u32[]{:S(2)}) copy-start(bf16[128,896]{1,0:T(8,128)(2,1)S(1)} %fusion.35) | copy-start | bytes 688132
  16.9 162.1 %all-gather.7.cloned.1.call-start = ((), (), s32[]{:S(2)}) async-start(), calls=%async_computation.3 | async-start | bytes 3899392 | tf_op jit(solution)/shard_map/all_gather | solution.py:24
  95.3 2.7 copy-start.17
  98.0 1.9 copy-start.6
  98.0 1.9 copy-start.16
  98.0 3.7 slice-start
  99.8 2.9 slice-start.1
  99.9 2.9 copy-start.25
  106.2 2.3 copy-start.7
  106.2 2.3 copy-start.13
  120.9 146.5 %reduce-scatter.2.cloned.1.call-start = ((), (), s32[]{:S(2)}) async-start(), calls=%async_computation.2 | async-start | bytes 3899392 | tf_op jit(solution)/shard_map/reduce_scatter | solution.py:100
  126.7 285.6 %all-reduce.5.cloned.1.call-start = ((), (), s32[]{:S(2)}) async-start(), calls=%async_computation.5 | async-start | bytes 4128768 | tf_op jit(solution)/shard_map/psum | solution.py:131
  183.2 2.2 copy-start.12
  183.2 2.5 copy-start.3
  183.2 3.8 copy-start.19
  183.2 3.8 copy-start.22
  184.5 3.7 copy-start.5
  185.8 4.4 copy-start.20
  185.8 4.4 copy-start.23
  190.0 496.7 %all-gather.9.cloned.1.call-start = ((), (), s32[]{:S(2)}) async-start(), calls=%async_computation.4 | async-start | bytes 27295744 | tf_op jit(solution)/shard_map/all_gather | solution.py:12
  192.1 5.0 copy-start.8
  192.1 9.7 %slice-start.2 = ((s8[7340032]{0:T(1024)(128)(4,1)}), s8[4194304]{0:T(1024)(128)(4,1)S(1)}, s32[]{:S(2)}) async-start(s8[7340032]{0:T(1024)(128)(4,1)} %bitcast.185), calls=%async_computation.8 | async-start | bytes 8388608
  197.1 4.7 slice-start.3
  197.1 4.7 copy-start.26
  201.8 65.6 %copy-start.10 = (bf16[128,896]{1,0:T(8,128)(2,1)S(1)}, bf16[128,896]{1,0:T(8,128)(2,1)}, u32[]{:S(2)}) copy-start(bf16[128,896]{1,0:T(8,128)(2,1)} %copy-done.9) | copy-start | bytes 688132
  (4 other events, 5.1 us)
Sparse Core Ops, SparseCore 0:
  17.0 75.3 all-gather.4
  121.0 57.9 all-gather.6
  183.4 83.9 reduce-scatter.1
  270.6 141.6 all-reduce.4
  414.5 272.1 all-gather.8
